TPU v7x, 32 devices: a whole 2x2x4 slice. The times are simulated.
32 devices in a mesh: dp: 2 (over x), tp: 4 (over z), cp: 4 (over y, core).
Axes of the slice: x: 2, y: 2, z: 4, core: 2. Of those that a mesh axis runs over, the one named last changes fastest.
Arguments:
- hidden: bfloat16 [4096, 2048], P(('dp', 'cp')), parts along dimension 0
- seg_ids: int32 [4096], P(('dp', 'cp')), parts along dimension 0
- w_q: bfloat16 [2048, 2048], P(None, 'tp')
- b_q: bfloat16 [2048], P('tp')
- w_kv: bfloat16 [2048, 256], replicated
- b_kv: bfloat16 [256], replicated
- w_o: bfloat16 [2048, 2048], P('tp')
- b_o: bfloat16 [2048], replicated
- ln_gain: bfloat16 [2048], replicated
- ln_bias: bfloat16 [2048], replicated
Outputs:
- output 1: bfloat16 [4096, 2048], P(('dp', 'cp')), parts along dimension 0
- output 2: bfloat16 [4096, 128], P(('dp', 'cp')), parts along dimension 0
- output 3: bfloat16 [4096, 128], P(('dp', 'cp')), parts along dimension 0
There are 2 independent parts. A program takes and returns all parts, laid end to end along the dimension named above; an argument that names none is the same for every part.
All inputs are finite; a program needn't handle non-finite values.
Results may differ from a plain program's by a relative error of at most 0.0128857.
Values are sent between devices in bfloat16 or wider.
A program may use at most 1 GiB of HBM per device.

v0:
```python
import jax
import jax.numpy as jnp
from jax import lax
from jax.sharding import PartitionSpec as P, NamedSharding

HEAD_DIM = 128
LN_EPS = 1e-5
ATTN_SCALE = HEAD_DIM ** -0.5


def layer_norm(x_blk, ln_gain, ln_bias):
    x_float = x_blk.astype(jnp.float32)
    centered = x_float - jnp.mean(x_float, axis=-1, keepdims=True)
    variance = jnp.mean(centered * centered, axis=-1, keepdims=True)
    return (centered * lax.rsqrt(variance + LN_EPS) * ln_gain.astype(jnp.float32) + ln_bias.astype(jnp.float32)).astype(jnp.bfloat16)


def merge_block(q_blk, k_blk, v_float, visible, m_prev, l_prev, acc_prev):
    scores = jnp.einsum('bhd,kd->bhk', q_blk, k_blk, preferred_element_type=jnp.float32) * ATTN_SCALE
    scores = jnp.where(visible[:, None, :], scores, -jnp.inf)
    m_new = jnp.maximum(m_prev, jnp.max(scores, axis=-1))
    p_weights = jnp.exp(scores - m_new[..., None])
    rescale = jnp.exp(m_prev - m_new)
    l_new = l_prev * rescale + jnp.sum(p_weights, axis=-1)
    acc_new = acc_prev * rescale[..., None] + jnp.einsum('bhk,kd->bhd', p_weights, v_float, preferred_element_type=jnp.float32)
    return m_new, l_new, acc_new


def solution(mesh):
    n_cp = mesh.shape['cp']
    send_pairs = [(i, i + 1) for i in range(n_cp - 1)]

    def local_block(hidden, seg_ids, w_q, b_q, w_kv, b_kv, w_o, b_o, ln_gain, ln_bias):
        tok_local = hidden.shape[0]
        heads_loc = w_q.shape[1] // HEAD_DIM
        q_rows = min(tok_local, 128)
        n_qblk = tok_local // q_rows
        normed = layer_norm(hidden, ln_gain, ln_bias)
        q_all = (jnp.dot(normed, w_q, preferred_element_type=jnp.float32) + b_q.astype(jnp.float32)).astype(jnp.bfloat16)
        kv_own = (jnp.dot(normed, w_kv, preferred_element_type=jnp.float32) + b_kv.astype(jnp.float32)).astype(jnp.bfloat16)
        q_blocks = q_all.reshape(n_qblk, q_rows, heads_loc, HEAD_DIM)
        seg_blocks = seg_ids.reshape(n_qblk, q_rows)
        pos_local = jnp.arange(tok_local, dtype=jnp.int32)
        pos_blocks = pos_local.reshape(n_qblk, q_rows)
        my_index = lax.axis_index('cp')

        def sweep_keys(kv_blk, seg_keys, causal, is_valid, soft_state):
            k_blk = kv_blk[:, :HEAD_DIM]
            v_float = kv_blk[:, HEAD_DIM:].astype(jnp.float32)

            def one_block(block_in):
                q_blk, seg_q, pos_q, m_prev, l_prev, acc_prev = block_in
                visible = (seg_keys[None, :] == seg_q[:, None]) & is_valid
                if causal:
                    visible = visible & (pos_local[None, :] <= pos_q[:, None])
                return merge_block(q_blk, k_blk, v_float, visible, m_prev, l_prev, acc_prev)

            return tuple(lax.map(one_block, (q_blocks, seg_blocks, pos_blocks) + tuple(soft_state)))

        m_init = jnp.full((n_qblk, q_rows, heads_loc), -1e30, jnp.float32)
        l_init = jnp.zeros((n_qblk, q_rows, heads_loc), jnp.float32)
        acc_init = jnp.zeros((n_qblk, q_rows, heads_loc, HEAD_DIM), jnp.float32)
        own_state = sweep_keys(kv_own, seg_ids, True, True, (m_init, l_init, acc_init))

        def shift_step(step_idx, loop_carry):
            kv_blk, seg_keys, m_prev, l_prev, acc_prev = loop_carry
            kv_blk = lax.ppermute(kv_blk, 'cp', send_pairs)
            seg_keys = lax.ppermute(seg_keys, 'cp', send_pairs)
            new_state = sweep_keys(kv_blk, seg_keys, False, my_index >= step_idx, (m_prev, l_prev, acc_prev))
            return (kv_blk, seg_keys) + new_state

        loop_out = lax.fori_loop(1, n_cp, shift_step, (kv_own, seg_ids) + own_state)
        attn_out = (loop_out[4] / loop_out[3][..., None]).astype(jnp.bfloat16).reshape(tok_local, heads_loc * HEAD_DIM)
        partial = jnp.dot(attn_out, w_o, preferred_element_type=jnp.float32).astype(jnp.bfloat16)
        proj_sum = lax.psum(partial, 'tp')
        y_out = (hidden.astype(jnp.float32) + proj_sum.astype(jnp.float32) + b_o.astype(jnp.float32)).astype(jnp.bfloat16)
        return y_out, kv_own[:, :HEAD_DIM], kv_own[:, HEAD_DIM:]

    row_spec = P(('dp', 'cp'), None)
    tok_spec = P(('dp', 'cp'))
    mapped = jax.shard_map(local_block, mesh=mesh,
                           in_specs=(row_spec, tok_spec, P(None, 'tp'), P('tp'), P(None, None), P(None), P('tp', None), P(None), P(None), P(None)),
                           out_specs=(row_spec, row_spec, row_spec), check_vma=False)
    return mapped
```

profile of v0, /device:TPU:0, one launch (start us, length us, event | category | flops | bytes accessed | tf_op | source)
XLA Modules:
  0.0 209.8 jit_solution(16017537299761667620)
XLA Ops:
  7.3 2.1 convert_reduce_fusion
  13.2 2.0 fusion.40
  15.3 2.0 reshape.183
  17.2 1.9 copy.15
  19.8 11.0 %while.67 = (s32[]{:T(128)}, f32[4,128,4]{1,2,0:T(4,128)S(1)}, f32[4,128,4]{1,2,0:T(4,128)}, f32[4,128,4,128]{3,1,2,0:T(8,128)S(1)}, s32[512]{0:T(512)S(1)}, /*i...) while((s32[]{:T(128)}, f32[4,128,4]{1,2,0:T(4,128)S(1)}, ...), condition=%wide.region_5.6_spmd.clone, body=%wide.region_2.5_spmd.clone.sunk | while | flops 136055296 | bytes 3962997 | solution.py:58
  19.9 1.3 fusion.71
  22.7 1.3 fusion.71
  25.4 1.3 fusion.71
  28.1 1.3 fusion.71
  31.5 74.4 %while.66 = (s32[]{:T(128)}, bf16[512,256]{1,0:T(8,128)(2,1)}, s32[512]{0:T(512)}, f32[4,128,4]{1,2,0:T(4,128)S(1)}, f32[4,128,4]{1,2,0:T(4,128)}, /*index=5*/f3...) while((s32[]{:T(128)}, bf16[512,256]{1,0:T(8,128)(2,1)}, ...), condition=%wide.region_11.12_spmd, body=%wide.region_6.11_spmd.sunk | while | flops 136054784 | bytes 6863788 | solution.py:72
  31.5 3.1 %collective-permute-start = (bf16[512,256]{1,0:T(8,128)(2,1)}, bf16[512,256]{1,0:T(8,128)(2,1)}, u32[]{:S(2)}, u32[]{:S(2)}) collective-permute-start(bf16[512,256]{1,0:T(8,128)(2,1)} %get-tuple-element.772), channel_id=1, source_target_pairs={{0,1},{1,2},{2,3},{4,5},{5,6},{6,7},{8,9},{9,10},{10,11},{12,13},{... | collective-permute-start | bytes 786440 | tf_op jit(solution)/shard_map/while/body/eval_jaxpr/ppermute | solution.py:67
  34.6 3.8 %collective-permute-start.1 = (s32[512]{0:T(512)}, s32[512]{0:T(512)S(1)}, u32[]{:S(2)}, u32[]{:S(2)}) collective-permute-start(s32[512]{0:T(512)} %get-tuple-element.773), channel_id=1, source_target_pairs={{0,1},{1,2},{2,3},{4,5},{5,6},{6,7},{8,9},{9,10},{10,11},{12,13},{... | collective-permute-start | bytes 6152 | tf_op jit(solution)/shard_map/while/body/eval_jaxpr/ppermute | solution.py:68
  40.8 13.8 %while.68 = (s32[]{:T(128)}, f32[4,128,4]{1,2,0:T(4,128)S(1)}, f32[4,128,4]{1,2,0:T(4,128)}, f32[4,128,4,128]{3,1,2,0:T(8,128)S(1)}, s32[512]{0:T(512)S(1)}, /*i...) while((s32[]{:T(128)}, f32[4,128,4]{1,2,0:T(4,128)S(1)}, ...), condition=%wide.region_10.10_spmd.clone, body=%wide.region_7.9_spmd.clone.sunk | while | flops 136054784 | bytes 4754046 | solution.py:58
  41.0 1.3 fusion.77
  43.0 1.3 constant_dynamic-update-slice_fusion.3
  44.4 1.3 fusion.77
  46.5 1.3 constant_dynamic-update-slice_fusion.3
  47.9 1.3 fusion.77
  49.9 1.3 constant_dynamic-update-slice_fusion.3
  51.3 1.3 fusion.77
  53.4 1.3 constant_dynamic-update-slice_fusion.3
  54.7 1.7 copy.66
  56.3 3.2 %collective-permute-start = (bf16[512,256]{1,0:T(8,128)(2,1)}, bf16[512,256]{1,0:T(8,128)(2,1)}, u32[]{:S(2)}, u32[]{:S(2)}) collective-permute-start(bf16[512,256]{1,0:T(8,128)(2,1)} %get-tuple-element.772), channel_id=1, source_target_pairs={{0,1},{1,2},{2,3},{4,5},{5,6},{6,7},{8,9},{9,10},{10,11},{12,13},{... | collective-permute-start | bytes 786440 | tf_op jit(solution)/shard_map/while/body/eval_jaxpr/ppermute | solution.py:67
  59.5 3.7 %collective-permute-start.1 = (s32[512]{0:T(512)}, s32[512]{0:T(512)S(1)}, u32[]{:S(2)}, u32[]{:S(2)}) collective-permute-start(s32[512]{0:T(512)} %get-tuple-element.773), channel_id=1, source_target_pairs={{0,1},{1,2},{2,3},{4,5},{5,6},{6,7},{8,9},{9,10},{10,11},{12,13},{... | collective-permute-start | bytes 6152 | tf_op jit(solution)/shard_map/while/body/eval_jaxpr/ppermute | solution.py:68
  65.6 13.8 %while.68 = (s32[]{:T(128)}, f32[4,128,4]{1,2,0:T(4,128)S(1)}, f32[4,128,4]{1,2,0:T(4,128)}, f32[4,128,4,128]{3,1,2,0:T(8,128)S(1)}, s32[512]{0:T(512)S(1)}, /*i...) while((s32[]{:T(128)}, f32[4,128,4]{1,2,0:T(4,128)S(1)}, ...), condition=%wide.region_10.10_spmd.clone, body=%wide.region_7.9_spmd.clone.sunk | while | flops 136054784 | bytes 4754046 | solution.py:58
  65.8 1.3 fusion.77
  69.2 1.3 fusion.77
  71.2 1.3 constant_dynamic-update-slice_fusion.3
  72.7 1.3 fusion.77
  74.7 1.3 constant_dynamic-update-slice_fusion.3
  76.1 1.3 fusion.77
  78.2 1.3 constant_dynamic-update-slice_fusion.3
  79.4 1.7 copy.66
  81.1 3.2 %collective-permute-start = (bf16[512,256]{1,0:T(8,128)(2,1)}, bf16[512,256]{1,0:T(8,128)(2,1)}, u32[]{:S(2)}, u32[]{:S(2)}) collective-permute-start(bf16[512,256]{1,0:T(8,128)(2,1)} %get-tuple-element.772), channel_id=1, source_target_pairs={{0,1},{1,2},{2,3},{4,5},{5,6},{6,7},{8,9},{9,10},{10,11},{12,13},{... | collective-permute-start | bytes 786440 | tf_op jit(solution)/shard_map/while/body/eval_jaxpr/ppermute | solution.py:67
  84.3 3.7 %collective-permute-start.1 = (s32[512]{0:T(512)}, s32[512]{0:T(512)S(1)}, u32[]{:S(2)}, u32[]{:S(2)}) collective-permute-start(s32[512]{0:T(512)} %get-tuple-element.773), channel_id=1, source_target_pairs={{0,1},{1,2},{2,3},{4,5},{5,6},{6,7},{8,9},{9,10},{10,11},{12,13},{... | collective-permute-start | bytes 6152 | tf_op jit(solution)/shard_map/while/body/eval_jaxpr/ppermute | solution.py:68
  90.4 13.8 %while.68 = (s32[]{:T(128)}, f32[4,128,4]{1,2,0:T(4,128)S(1)}, f32[4,128,4]{1,2,0:T(4,128)}, f32[4,128,4,128]{3,1,2,0:T(8,128)S(1)}, s32[512]{0:T(512)S(1)}, /*i...) while((s32[]{:T(128)}, f32[4,128,4]{1,2,0:T(4,128)S(1)}, ...), condition=%wide.region_10.10_spmd.clone, body=%wide.region_7.9_spmd.clone.sunk | while | flops 136054784 | bytes 4754046 | solution.py:58
  90.5 1.3 fusion.77
  92.6 1.3 constant_dynamic-update-slice_fusion.3
  94.0 1.3 fusion.77
  96.0 1.3 constant_dynamic-update-slice_fusion.3
  97.4 1.3 fusion.77
  99.5 1.3 constant_dynamic-update-slice_fusion.3
  100.9 1.3 fusion.77
  102.9 1.3 constant_dynamic-update-slice_fusion.3
  104.2 1.7 copy.66
  107.4 2.6 %convolution_convert_fusion = bf16[512,2048]{1,0:T(8,128)(2,1)} fusion(bf16[512,2048]{1,0:T(8,128)(2,1)S(1)} %copy-done, bf16[64,8,4,128]{3,2,1,0:T(4,128)(2,1)S(1)} %bitcast.114), kind=kOutput, calls=%fused_computation.68 | convolution fusion | flops 1074790400 | bytes 4718592 | tf_op jit(solution)/shard_map/dot_general | solution.py:74
  110.6 87.8 %all-reduce.2.cloned.1.call-done = bf16[512,2048]{1,0:T(8,128)(2,1)} async-done(((bf16[512,2048]{1,0:T(8,128)(2,1)}), bf16[512,2048]{1,0:T(8,128)(2,1)}) %all-reduce.2.cloned.1.call-update) | async-done | bytes 2097168 | tf_op jit(solution)/shard_map/psum | solution.py:75
  198.5 4.5 %fusion.39 = bf16[512,2048]{1,0:T(8,128)(2,1)} fusion(bf16[512,2048]{1,0:T(8,128)(2,1)} %param.16, bf16[512,2048]{1,0:T(8,128)(2,1)} %all-reduce.2.cloned.1.call-done, f32[2048]{0:T(1024)S(1)} %convert_element_type.62), kind=kLoop, calls=%fused_computation.67 | loop fusion | flops 5242880 | bytes 6299648 | tf_op jit(solution)/shard_map/convert_element_type | solution.py:76
  (155 shorter events, 31.5 us)
Async XLA Ops:
  7.2 100.2 %copy-start = (bf16[512,2048]{1,0:T(8,128)(2,1)S(1)}, bf16[512,2048]{1,0:T(8,128)(2,1)}, u32[]{:S(2)}) copy-start(bf16[512,2048]{1,0:T(8,128)(2,1)} %param.22) | copy-start | bytes 6291460
  7.2 191.3 %all-reduce.2.cloned.1.call-start = ((), (), s32[]{:S(2)}) async-start(), calls=%async_computation | async-start | bytes 4194304 | tf_op jit(solution)/shard_map/psum | solution.py:75
  7.3 2.4 %copy-start.1 = (bf16[512,2048]{1,0:T(8,128)(2,1)S(1)}, bf16[512,2048]{1,0:T(8,128)(2,1)}, u32[]{:S(2)}) copy-start(bf16[512,2048]{1,0:T(8,128)(2,1)} %param.16) | copy-start | bytes 6291460
  7.3 3.0 %copy-start.6 = (bf16[2048]{0:T(1024)(128)(2,1)S(1)}, bf16[2048]{0:T(1024)(128)(2,1)}, u32[]{:S(2)}) copy-start(bf16[2048]{0:T(1024)(128)(2,1)} %param.24) | copy-start | bytes 12292
  7.3 3.0 %copy-start.7 = (bf16[2048]{0:T(1024)(128)(2,1)S(1)}, bf16[2048]{0:T(1024)(128)(2,1)}, u32[]{:S(2)}) copy-start(bf16[2048]{0:T(1024)(128)(2,1)} %param.25) | copy-start | bytes 12292
  7.3 3.1 %copy-start.12 = (bf16[256]{0:T(256)(128)(2,1)S(1)}, bf16[256]{0:T(256)(128)(2,1)}, u32[]{:S(2)}) copy-start(bf16[256]{0:T(256)(128)(2,1)} %param.21) | copy-start | bytes 1540
  10.4 1.2 copy-start.11
  11.6 1.5 copy-start.9
  11.6 1.6 copy-start.10
  12.3 0.7 copy-start.4
  15.3 3.9 %copy-start.5 = (s32[512]{0:T(512)S(1)}, s32[512]{0:T(512)}, u32[]{:S(2)}) copy-start(s32[512]{0:T(512)} %param.17) | copy-start | bytes 6148
  30.8 0.7 copy-start.3
  30.8 0.7 copy-start.2
  31.5 8.4 %collective-permute-start = (bf16[512,256]{1,0:T(8,128)(2,1)}, bf16[512,256]{1,0:T(8,128)(2,1)}, u32[]{:S(2)}, u32[]{:S(2)}) collective-permute-start(bf16[512,256]{1,0:T(8,128)(2,1)} %get-tuple-element.772), channel_id=1, source_target_pairs={{0,1},{1,2},{2,3},{4,5},{5,6},{6,7},{8,9},{9,10},{10,11},{12,13},{... | collective-permute-start | bytes 786440 | tf_op jit(solution)/shard_map/while/body/eval_jaxpr/ppermute | solution.py:67
  34.6 4.6 %collective-permute-start.1 = (s32[512]{0:T(512)}, s32[512]{0:T(512)S(1)}, u32[]{:S(2)}, u32[]{:S(2)}) collective-permute-start(s32[512]{0:T(512)} %get-tuple-element.773), channel_id=1, source_target_pairs={{0,1},{1,2},{2,3},{4,5},{5,6},{6,7},{8,9},{9,10},{10,11},{12,13},{... | collective-permute-start | bytes 6152 | tf_op jit(solution)/shard_map/while/body/eval_jaxpr/ppermute | solution.py:68
  56.3 8.3 %collective-permute-start = (bf16[512,256]{1,0:T(8,128)(2,1)}, bf16[512,256]{1,0:T(8,128)(2,1)}, u32[]{:S(2)}, u32[]{:S(2)}) collective-permute-start(bf16[512,256]{1,0:T(8,128)(2,1)} %get-tuple-element.772), channel_id=1, source_target_pairs={{0,1},{1,2},{2,3},{4,5},{5,6},{6,7},{8,9},{9,10},{10,11},{12,13},{... | collective-permute-start | bytes 786440 | tf_op jit(solution)/shard_map/while/body/eval_jaxpr/ppermute | solution.py:67
  59.5 4.5 %collective-permute-start.1 = (s32[512]{0:T(512)}, s32[512]{0:T(512)S(1)}, u32[]{:S(2)}, u32[]{:S(2)}) collective-permute-start(s32[512]{0:T(512)} %get-tuple-element.773), channel_id=1, source_target_pairs={{0,1},{1,2},{2,3},{4,5},{5,6},{6,7},{8,9},{9,10},{10,11},{12,13},{... | collective-permute-start | bytes 6152 | tf_op jit(solution)/shard_map/while/body/eval_jaxpr/ppermute | solution.py:68
  81.1 8.3 %collective-permute-start = (bf16[512,256]{1,0:T(8,128)(2,1)}, bf16[512,256]{1,0:T(8,128)(2,1)}, u32[]{:S(2)}, u32[]{:S(2)}) collective-permute-start(bf16[512,256]{1,0:T(8,128)(2,1)} %get-tuple-element.772), channel_id=1, source_target_pairs={{0,1},{1,2},{2,3},{4,5},{5,6},{6,7},{8,9},{9,10},{10,11},{12,13},{... | collective-permute-start | bytes 786440 | tf_op jit(solution)/shard_map/while/body/eval_jaxpr/ppermute | solution.py:67
  84.3 4.5 %collective-permute-start.1 = (s32[512]{0:T(512)}, s32[512]{0:T(512)S(1)}, u32[]{:S(2)}, u32[]{:S(2)}) collective-permute-start(s32[512]{0:T(512)} %get-tuple-element.773), channel_id=1, source_target_pairs={{0,1},{1,2},{2,3},{4,5},{5,6},{6,7},{8,9},{9,10},{10,11},{12,13},{... | collective-permute-start | bytes 6152 | tf_op jit(solution)/shard_map/while/body/eval_jaxpr/ppermute | solution.py:68
  109.9 0.7 copy-start.8
Sparse Core Ops, SparseCore 0:
  110.1 88.3 all-reduce.1
where the time goes:
time: 211 us; the launch traced here: 210 us
  waiting for transfers between devices  90.2 us (43%)
  other arithmetic  34.2 us (16%)
  matrix products  31.9 us (15%)
  starting transfers between devices  20.7 us (10%)
  local copies, waits for them, and re-layouts  17.9 us (8%)
  between operations  14.2 us (7%)
    psum x1, waiting for transfers between devices, local_block(): proj_sum = lax.psum(partial, 'tp')  87.8 us
    dot_general x16, matrix products, merge_block(): jnp.einsum('bhd,kd->bhk', q_blk, k_blk, preferred_element_type=jnp.float32)  20.8 us
    dynamic_update_slice x16, other arithmetic, sweep_keys(): lax.map(one_block, (q_blocks, seg_blocks, pos_blocks) + tuple(soft_state))  17.7 us
    ppermute x3, starting transfers between devices, shift_step(): seg_keys = lax.ppermute(seg_keys, 'cp', send_pairs)  11.2 us
    ppermute x3, starting transfers between devices, shift_step(): kv_blk = lax.ppermute(kv_blk, 'cp', send_pairs)  9.48 us
    while x6, local copies, waits for them, and re-layouts  6.79 us
    dot_general x16, matrix products, merge_block(): jnp.einsum('bhk,kd->bhd', p_weights, v_float, preferred_element_type=jnp....  5.75 us
    reduce_sum x16, other arithmetic, merge_block(): l_new = l_prev * rescale + jnp.sum(p_weights, axis=-1)  5.34 us
  transfers between devices with their start and end apart: 7, of which 4 were waited for; matrix products, arithmetic and copies ran while one was open for 1% of the time, Pallas kernels for 0%

commit v1 on v0

v1 whole, which is shorter than its diff:
```python
import functools
import jax
import jax.numpy as jnp
from jax import lax
from jax.experimental import pallas as pl
from jax.experimental.pallas import tpu as pltpu
from jax.sharding import PartitionSpec as P

HEAD_DIM = 128
LN_EPS = 1e-5
SCORE_SCALE = HEAD_DIM ** -0.5 * 1.4426950408889634
MESH = pl.DeviceIdType.MESH
BF16 = jnp.bfloat16
F32 = jnp.float32


class Sends:
    def __init__(self, sems):
        self.sems, self.made = sems, []

    def go(self, src, dst, recv, to, cond=None):
        slot = len(self.made)
        make = lambda: pltpu.make_async_remote_copy(src_ref=src(), dst_ref=dst(), send_sem=self.sems.at[slot], recv_sem=recv(),
                                                    device_id=to, device_id_type=MESH)
        self.made.append((make, cond))
        if cond is None:
            make().start()
        else:
            pl.when(cond())(lambda: make().start())

    def finish(self):
        for make, cond in self.made:
            if cond is None:
                make().wait_send()
            else:
                pl.when(cond())(lambda: make().wait_send())


def arrived(dst, recv):
    pltpu.make_async_copy(dst, dst, recv).wait()


N_SENDS = 64


def kernel(hid_hbm, seg_hbm, wq_hbm, bq_hbm, wkv_hbm, bkv_ref, wo_hbm, bo_ref, gain_ref, lnb_ref,
           y_ref, k_ref, v_ref,
           hid, normed, wkv, wq, wo, bq, seg, segcol, kv, q_s, o_all, part, m_s, l_s, acc_s,
           load_sem, send_sem, o_send, bq_recv, seg_recv, kv_recv, wq_recv, wo_recv, o_recv):
    tok, d_model = hid.shape
    width = wq.shape[2]
    heads = width // HEAD_DIM
    tile = tok // 4
    q_rows, o_rows = d_model // 8, width // 8
    dp, z, cp = lax.axis_index('dp'), lax.axis_index('tp'), lax.axis_index('cp')
    y, c = cp // 2, cp % 2
    pair = z + 1 - 2 * (z % 2)
    below, above = {'tp': z - 1}, {'tp': z + 1}
    to_x, to_y, to_core = {'dp': 1 - dp}, {'cp': cp + 2 - 4 * y}, {'cp': cp + 1 - 2 * c}
    pos = lambda px, py, pc: px * 4 + py * 2 + pc
    p_me, p_x, p_y, p_d = pos(dp, y, c), pos(1 - dp, y, c), pos(dp, 1 - y, c), pos(1 - dp, 1 - y, c)
    g_a = 1 + z % 2
    g_c = 3 - 3 * (z // 2)
    g_b = 6 - z - g_a - g_c
    sends = Sends(send_sem)

    loads = [pltpu.make_async_copy(hid_hbm, hid, load_sem.at[0]),
             pltpu.make_async_copy(wkv_hbm, wkv, load_sem.at[1]),
             pltpu.make_async_copy(wq_hbm, wq.at[0], load_sem.at[2]),
             pltpu.make_async_copy(bq_hbm, bq.at[0], load_sem.at[3]),
             pltpu.make_async_copy(seg_hbm, seg.at[cp], load_sem.at[4]),
             pltpu.make_async_copy(wo_hbm, wo.at[pl.ds(z * width, width), :], load_sem.at[5])]
    for load in loads:
        load.start()

    barrier = pltpu.get_barrier_semaphore()
    for step in (1, 2, 3):
        pl.semaphore_signal(barrier, inc=1, device_id={'cp': (cp + step) % 4}, device_id_type=MESH)
    pl.semaphore_signal(barrier, inc=1, device_id=to_x, device_id_type=MESH)

    @pl.when(z > 0)
    def _():
        pl.semaphore_signal(barrier, inc=1, device_id={'tp': z - 1}, device_id_type=MESH)

    @pl.when(z < 3)
    def _():
        pl.semaphore_signal(barrier, inc=1, device_id={'tp': z + 1}, device_id_type=MESH)

    pl.semaphore_wait(barrier, 5 + (z + 1) // 2 - 2 * (z // 3))

    wq_piece = lambda p: wq.at[1, pl.ds(p * q_rows, q_rows), :]
    wo_piece = lambda g, p: wo.at[pl.ds(g * width + p * o_rows, o_rows), :]

    own_q, own_o = lambda: wq_hbm.at[pl.ds(p_me * q_rows, q_rows), :], lambda: wo_hbm.at[pl.ds(p_me * o_rows, o_rows), :]
    sends.go(lambda: bq_hbm, lambda: bq.at[1], lambda: bq_recv, {'tp': pair})
    sends.go(own_q, lambda: wq_piece(p_me), lambda: wq_recv.at[p_me], {'tp': pair})
    sends.go(own_o, lambda: wo_piece(z, p_me), lambda: wo_recv.at[z, p_me], {'tp': z - 1}, lambda: z > 0)
    sends.go(own_o, lambda: wo_piece(z, p_me), lambda: wo_recv.at[z, p_me], {'tp': z + 1}, lambda: z < 3)
    for step in (1, 2, 3):
        sends.go(lambda: seg_hbm, lambda: seg.at[cp], lambda: seg_recv.at[cp], {'cp': cp + step}, lambda step=step: cp + step < 4)

    def pass_on(piece, recv, source, g=None):
        p = {'z': p_me, 'x': p_x, 'y': p_y, 'd': p_d}[source]
        src, sem = lambda: piece(p), lambda: recv(p)
        arrived(src(), sem())
        if source == 'z':
            if g is not None:
                sends.go(src, src, sem, below, lambda: (g > z) & (z > 0))
                sends.go(src, src, sem, above, lambda: (g < z) & (z < 3))
            sends.go(src, src, sem, to_x)
            sends.go(src, src, sem, to_y)
        elif source == 'x':
            sends.go(src, src, sem, to_y, lambda: c == 1)
        elif source == 'y':
            sends.go(src, src, sem, to_x, lambda: c == 0)
        sends.go(src, src, sem, to_core)

    def from_core(piece, recv):
        for px in (0, 1):
            for py in (0, 1):
                p = pos(px, py, 1 - c)
                arrived(piece(p), recv(p))

    def q_event(*sources):
        for source in sources:
            pass_on(wq_piece, lambda p: wq_recv.at[p], source)

    def o_event(g, *sources):
        for source in sources:
            pass_on(functools.partial(wo_piece, g), lambda p: wo_recv.at[g, p], source, g)

    loads[0].wait()
    gain = gain_ref[...].astype(F32)
    lnb = lnb_ref[...].astype(F32)
    ln_rows = min(64, tok)

    def ln_step(i, carry):
        rows = pl.ds(pl.multiple_of(i * ln_rows, ln_rows), ln_rows)
        x = hid[rows, :].astype(F32)
        cen = x - jnp.mean(x, axis=-1, keepdims=True)
        var = jnp.mean(cen * cen, axis=-1, keepdims=True)
        normed[rows, :] = (cen * lax.rsqrt(var + LN_EPS) * gain + lnb).astype(BF16)
        return carry

    lax.fori_loop(0, tok // ln_rows, ln_step, 0)

    loads[1].wait()
    kv_new = (jnp.dot(normed[...], wkv[...], preferred_element_type=F32) + bkv_ref[...].astype(F32)).astype(BF16)
    kv[cp, 0] = kv_new[:, :HEAD_DIM]
    kv[cp, 1] = kv_new[:, HEAD_DIM:]
    k_ref[...] = kv_new[:, :HEAD_DIM]
    v_ref[...] = kv_new[:, HEAD_DIM:]

    def project_q(which):
        qf = jnp.dot(normed[...], wq[which], preferred_element_type=F32) + bq[which].astype(F32)
        for r in range(4):
            for h in range(heads):
                q_s[which * 4 + r, h * tile:(h + 1) * tile, :] = qf[r * tile:(r + 1) * tile, h * HEAD_DIM:(h + 1) * HEAD_DIM].astype(BF16)

    loads[2].wait()
    loads[3].wait()
    sends.go(lambda: kv.at[cp], lambda: kv.at[cp], lambda: kv_recv.at[cp], to_core, lambda: c == 0)
    sends.go(lambda: kv.at[cp], lambda: kv.at[cp], lambda: kv_recv.at[cp], to_y, lambda: y == 0)
    project_q(0)
    loads[4].wait()
    for r in range(4):
        row = jnp.broadcast_to(seg[cp, :, r * tile:(r + 1) * tile], (tile, tile))
        segcol[r] = row.T

    @pl.when(y == 1)
    def _():
        arrived(kv.at[c], kv_recv.at[c])

    sends.go(lambda: kv.at[c], lambda: kv.at[c], lambda: kv_recv.at[c], to_core, lambda: y == 1)
    q_event('z')

    def scores(q, k_blk, mask):
        s = lax.dot_general(q, k_blk, (((1,), (1,)), ((), ())), preferred_element_type=F32) * SCORE_SCALE
        keys = k_blk.shape[0]
        return jnp.where(mask[None], s.reshape(heads, tile, keys), -jnp.inf).reshape(heads * tile, keys)

    def attend(t, carry):
        r = t % 4
        g = jnp.where(t < 4, z, pair)

        @pl.when(t == 4)
        def _():
            from_core(wq_piece, lambda p: wq_recv.at[p])
            arrived(bq.at[1], bq_recv)
            project_q(1)

        q = q_s[t]
        seg_q = segcol[r][:, :1]
        k_pos = lax.broadcasted_iota(jnp.int32, (tile, tok), 1)
        q_pos = lax.broadcasted_iota(jnp.int32, (tile, tok), 0) + r * tile
        s = scores(q, kv[cp, 0], (seg[cp] == seg_q) & (k_pos <= q_pos))
        m_new = jnp.max(s, axis=-1, keepdims=True)
        p = jnp.exp2(s - m_new)
        m_s[...] = jnp.broadcast_to(m_new, m_s.shape)
        l_s[...] = jnp.broadcast_to(jnp.sum(p, axis=-1, keepdims=True), l_s.shape)
        acc_s[...] = jnp.dot(p.astype(BF16), kv[cp, 1], preferred_element_type=F32)

        @pl.when(t == 0)
        def _():
            for j in range(3):
                pl.when(j < cp)(functools.partial(arrived, seg.at[j], seg_recv.at[j]))
            pl.when(y == 1)(functools.partial(arrived, kv.at[1 - c], kv_recv.at[1 - c]))
            pl.when(c == 1)(functools.partial(arrived, kv.at[cp - 1], kv_recv.at[cp - 1]))

        def earlier(j, inner):
            s = scores(q, kv[j, 0], seg[j] == seg_q)
            m_prev = m_s[...]
            m_new = jnp.maximum(m_prev, jnp.max(s, axis=-1, keepdims=True))
            p = jnp.exp2(s - m_new[:, :1])
            alpha = jnp.exp2(m_prev - m_new)
            m_s[...] = m_new
            l_s[...] = l_s[...] * alpha + jnp.sum(p, axis=-1, keepdims=True)
            acc_s[...] = acc_s[...] * alpha + jnp.dot(p.astype(BF16), kv[j, 1], preferred_element_type=F32)
            return inner

        lax.fori_loop(0, cp, earlier, 0)
        rows = pl.ds(pl.multiple_of(r * tile, tile), tile)
        for h in range(heads):
            part_o = acc_s[h * tile:(h + 1) * tile, :] / l_s[h * tile:(h + 1) * tile, :]
            o_all[g, rows, h * HEAD_DIM:(h + 1) * HEAD_DIM] = part_o.astype(BF16)

        events = {0: [(o_event, g_a, 'z')], 1: [(q_event, 'x', 'y')], 2: [(o_event, g_b, 'z')], 3: [(q_event, 'd')],
                  4: [(o_event, g_a, 'x', 'y')], 5: [(o_event, g_c, 'z'), (o_event, g_a, 'd')], 6: [(o_event, g_b, 'x', 'y')],
                  7: [(o_event, g_b, 'd')]}
        for when, todo in events.items():
            @pl.when(t == when)
            def _():
                for what, *about in todo:
                    what(*about)

        o_tile = o_all.at[g, rows, :]
        copy = pltpu.make_async_remote_copy(src_ref=o_tile, dst_ref=o_tile, send_sem=o_send.at[t], recv_sem=o_recv.at[t],
                                            device_id={'tp': 3 - z}, device_id_type=MESH)
        pl.when((z > 0) & (z < 3))(lambda: copy.start())
        return carry

    lax.fori_loop(0, 8, attend, 0)

    n_col = min(512, d_model)

    def project_o(g, rows, n_rows):
        def cols(n, carry):
            at = pl.ds(pl.multiple_of(n * n_col, n_col), n_col)
            part[g, rows, at] = jnp.dot(o_all[g, rows, :], wo[pl.ds(pl.multiple_of(g * width, width), width), at],
                                        preferred_element_type=F32).astype(BF16)
            return carry

        lax.fori_loop(0, d_model // n_col, cols, 0)

    loads[5].wait()
    every = pl.ds(0, tok)
    project_o(z, every, tok)
    from_core(functools.partial(wo_piece, g_a), lambda p: wo_recv.at[g_a, p])
    from_core(functools.partial(wo_piece, g_b), lambda p: wo_recv.at[g_b, p])
    project_o(pair, every, tok)

    def other(u, carry):
        r = u % 4
        g_1, g_2 = 2 - z // 2, 3 - 3 * (z // 2)
        g = jnp.where(u < 4, g_1, g_2)
        rows = pl.ds(pl.multiple_of(r * tile, tile), tile)
        o_tile = o_all.at[g, rows, :]
        arrived(o_tile, o_recv.at[u])
        for edge, cond in ((0, z == 1), (3, z == 2)):
            copy = pltpu.make_async_remote_copy(src_ref=o_tile, dst_ref=o_tile, send_sem=o_send.at[8 + u], recv_sem=o_recv.at[u],
                                                device_id={'tp': edge}, device_id_type=MESH)
            pl.when(cond)(lambda copy=copy: copy.start())

        @pl.when(u == 2)
        def _():
            o_event(g_c, 'x', 'y')

        @pl.when(u == 3)
        def _():
            o_event(g_c, 'd')
            from_core(functools.partial(wo_piece, g_c), lambda p: wo_recv.at[g_c, p])

        project_o(g, rows, tile)

        @pl.when(u >= 4)
        def _():
            def finish(i, inner):
                f_rows = tile // 4
                at = pl.ds(pl.multiple_of(r * tile + i * f_rows, f_rows), f_rows)
                total = part[0, at, :].astype(F32)
                for gg in (1, 2, 3):
                    total = total + part[gg, at, :].astype(F32)
                y_ref[at, :] = (hid[at, :].astype(F32) + total + bo_ref[...].astype(F32)).astype(BF16)
                return inner

            lax.fori_loop(0, 4, finish, 0)

        return carry

    lax.fori_loop(0, 8, other, 0)

    sends.finish()

    @pl.when((z > 0) & (z < 3))
    def _():
        def sent(u, carry):
            g = jnp.where(u < 4, z, pair)
            g_1, g_2 = 2 - z // 2, 3 - 3 * (z // 2)
            rows = pl.ds(pl.multiple_of((u % 4) * tile, tile), tile)
            for which, gg in ((u, g), (u + 8, jnp.where(u < 4, g_1, g_2))):
                o_tile = o_all.at[gg, rows, :]
                pltpu.make_async_copy(o_tile, o_tile, o_send.at[which]).wait()
            return carry

        lax.fori_loop(0, 8, sent, 0)


def solution(mesh):
    def local_block(hidden, seg_ids, w_q, b_q, w_kv, b_kv, w_o, b_o, ln_gain, ln_bias):
        tok, d_model = hidden.shape
        width = w_q.shape[1]
        heads = width // HEAD_DIM
        tile = tok // 4
        hbm = pl.BlockSpec(memory_space=pl.ANY)
        vmem = pl.BlockSpec(memory_space=pltpu.VMEM)
        row = lambda a: a.reshape(1, -1)
        dma = pltpu.SemaphoreType.DMA
        return pl.pallas_call(
            kernel,
            out_shape=(jax.ShapeDtypeStruct((tok, d_model), BF16), jax.ShapeDtypeStruct((tok, HEAD_DIM), BF16),
                       jax.ShapeDtypeStruct((tok, HEAD_DIM), BF16)),
            in_specs=[hbm, hbm, hbm, hbm, hbm, vmem, hbm, vmem, vmem, vmem],
            out_specs=(vmem, vmem, vmem),
            scratch_shapes=[
                pltpu.VMEM((tok, d_model), BF16),
                pltpu.VMEM((tok, d_model), BF16),
                pltpu.VMEM((d_model, 2 * HEAD_DIM), BF16),
                pltpu.VMEM((2, d_model, width), BF16),
                pltpu.VMEM((4 * width, d_model), BF16),
                pltpu.VMEM((2, 1, width), BF16),
                pltpu.VMEM((4, 1, tok), jnp.int32),
                pltpu.VMEM((4, tile, tile), jnp.int32),
                pltpu.VMEM((4, 2, tok, HEAD_DIM), BF16),
                pltpu.VMEM((8, heads * tile, HEAD_DIM), BF16),
                pltpu.VMEM((4, tok, width), BF16),
                pltpu.VMEM((4, tok, d_model), BF16),
                pltpu.VMEM((heads * tile, HEAD_DIM), F32),
                pltpu.VMEM((heads * tile, HEAD_DIM), F32),
                pltpu.VMEM((heads * tile, HEAD_DIM), F32),
                dma((6,)), dma((N_SENDS,)), dma((16,)), dma(()), dma((4,)), dma((4,)), dma((8,)), dma((4, 8)), dma((8,)),
            ],
            compiler_params=pltpu.CompilerParams(collective_id=0, has_side_effects=True, vmem_limit_bytes=60 * 2 ** 20),
            name='block',
        )(hidden, row(seg_ids), w_q, row(b_q), w_kv, row(b_kv), w_o, row(b_o), row(ln_gain), row(ln_bias))

    row_spec = P(('dp', 'cp'), None)
    tok_spec = P(('dp', 'cp'))
    return jax.shard_map(local_block, mesh=mesh,
                         in_specs=(row_spec, tok_spec, P(None, 'tp'), P('tp'), P(None, None), P(None), P('tp', None), P(None), P(None), P(None)),
                         out_specs=(row_spec, row_spec, row_spec), check_vma=False)
```

time: 211 us -> 95.2 us (0.45)
  waiting for transfers between devices: 90.2 us -> 0 us
  Pallas kernels: 0 us -> 83.3 us
  other arithmetic: 34.2 us -> 0 us
  matrix products: 31.9 us -> 0 us
  starting transfers between devices: 20.7 us -> 0 us
  between operations: 14.2 us -> 0.66 us
  local copies, waits for them, and re-layouts: 17.9 us -> 10.9 us
    psum x1 -> x0, waiting for transfers between devices: 87.8 us -> none  [local_block(): proj_sum = lax.psum(partial, 'tp')]
    pallas_call x0 -> x1, Pallas kernels: none -> 83.3 us  [local_block(): pl.pallas_call(kernel, out_shape=(jax.ShapeDtypeStruct((tok, d_model), BF...]
    dot_general x35 -> x0, matrix products: 31.9 us -> none  [the longest x16 20.8 us: merge_block(): jnp.einsum('bhd,kd->bhk', q_blk, k_blk, preferred_element_type=jnp.float32)]
    ppermute x6 -> x0, starting transfers between devices: 20.7 us -> none  [the longest x3 11.2 us: shift_step(): seg_keys = lax.ppermute(seg_keys, 'cp', send_pairs)]
    dynamic_update_slice x16 -> x0, other arithmetic: 17.7 us -> none  [sweep_keys(): lax.map(one_block, (q_blocks, seg_blocks, pos_blocks) + tuple(soft_state))]
    reduce_sum x18 -> x0, other arithmetic: 8.11 us -> none  [the longest x16 5.34 us: merge_block(): l_new = l_prev * rescale + jnp.sum(p_weights, axis=-1)]
    while x6 -> x0, local copies, waits for them, and re-layouts: 6.79 us -> none
    convert_element_type x8 -> x0, other arithmetic: 6.39 us -> none  [the longest x1 4.5 us: local_block(): (hidden.astype(jnp.float32) + proj_sum.astype(jnp.float32) + b_o.astype(j...]
  transfers between devices with their start and end apart: 7 -> 0, of which waited for: 4 -> 0; matrix products, arithmetic and copies ran while one was open for 1% -> 0% of each run, Pallas kernels for 0% -> 0%
where the time goes in v1:
time: 95.2 us; the launch traced here: 94.9 us
  Pallas kernels  83.3 us (88%)
  local copies, waits for them, and re-layouts  10.9 us (11%)
    pallas_call x1, Pallas kernels, local_block(): pl.pallas_call(kernel, out_shape=(jax.ShapeDtypeStruct((tok, d_model), BF...  83.3 us
    reshape x5, local copies, waits for them, and re-layouts, local_block(): row = lambda a: a.reshape(1, -1)  6.36 us
    unnamed x7, local copies, waits for them, and re-layouts  4.52 us

profile of v1, /device:TPU:0, one launch (start us, length us, event | category | flops | bytes accessed | tf_op | source)
XLA Modules:
  0.0 94.9 jit_solution(6869930550459312459)
XLA Ops:
  0.6 1.2 %reshape.26.bkv_ref = bf16[1,256]{1,0:T(2,128)(2,1)} reshape(bf16[256]{0:T(256)(128)(2,1)} %param.15) | data formatting | bytes 1024 | tf_op jit(solution)/shard_map/reshape | solution.py:326
  1.9 1.3 %reshape.25.bq_hbm = bf16[1,512]{1,0:T(2,128)(2,1)} reshape(bf16[512]{0:T(512)(128)(2,1)} %param.13) | data formatting | bytes 2048 | tf_op jit(solution)/shard_map/reshape | solution.py:326
  3.1 1.3 %reshape.27.bo_ref = bf16[1,2048]{1,0:T(2,128)(2,1)} reshape(bf16[2048]{0:T(1024)(128)(2,1)} %param.17) | data formatting | bytes 8192 | tf_op jit(solution)/shard_map/reshape | solution.py:326
  4.4 1.3 %reshape.28.gain_ref = bf16[1,2048]{1,0:T(2,128)(2,1)} reshape(bf16[2048]{0:T(1024)(128)(2,1)} %param.18) | data formatting | bytes 8192 | tf_op jit(solution)/shard_map/reshape | solution.py:326
  5.7 1.3 %reshape.29.lnb_ref = bf16[1,2048]{1,0:T(2,128)(2,1)} reshape(bf16[2048]{0:T(1024)(128)(2,1)} %param.19) | data formatting | bytes 8192 | tf_op jit(solution)/shard_map/reshape | solution.py:326
  7.0 83.3 %block.1 = (bf16[512,2048]{1,0:T(8,128)(2,1)}, bf16[512,128]{1,0:T(8,128)(2,1)}, bf16[512,128]{1,0:T(8,128)(2,1)}) custom-call(bf16[512,2048]{1,0:T(8,128)(2,1)} %hid_hbm.1, s32[1,512]{1,0:T(1,128)} %bitcast.1, bf16[2048,512]{1,0:T(8,128)(2,1)} %wq_hbm.1, bf16[1,512]{1,0:T(2,128)(2,1)} %reshape.25.bq_hbm, bf16[2048,256]{1,0:T(8,128)(2,1)} %wkv_hbm.1, ...), custom_call_target="tpu_custom_call" | custom-call | tf_op jit(solution)/shard_map/block/pallas_call | solution.py:328
  90.3 0.0 copy-start.1
  90.3 0.0 copy-start
  90.3 3.2 %copy.16 = bf16[512,2048]{1,0:T(8,128)(2,1)} copy(bf16[512,2048]{1,0:T(8,128)(2,1)} %get-tuple-element.6) | data formatting | bytes 4194304
  93.5 0.0 copy-done.1
  93.5 0.7 copy.17
  94.2 0.0 copy-done
  94.2 0.7 copy.18
Async XLA Ops:
  90.3 3.2 %copy-start.1 = (bf16[512,128]{1,0:T(8,128)(2,1)S(1)}, bf16[512,128]{1,0:T(8,128)(2,1)}, u32[]{:S(2)}) copy-start(bf16[512,128]{1,0:T(8,128)(2,1)} %get-tuple-element.7) | copy-start | bytes 393220
  90.3 3.9 %copy-start = (bf16[512,128]{1,0:T(8,128)(2,1)S(1)}, bf16[512,128]{1,0:T(8,128)(2,1)}, u32[]{:S(2)}) copy-start(bf16[512,128]{1,0:T(8,128)(2,1)} %get-tuple-element.8) | copy-start | bytes 393220

commit v2 on v1

--- a/solution.py
+++ b/solution.py
@@ -43,9 +43,9 @@
 N_SENDS = 64
 
 
-def kernel(hid_hbm, seg_hbm, wq_hbm, bq_hbm, wkv_hbm, bkv_ref, wo_hbm, bo_ref, gain_ref, lnb_ref,
+def kernel(hid_hbm, seg_hbm, wq_hbm, bq_hbm, wkv_hbm, bkv_hbm, wo_hbm, bo_hbm, gain_hbm, lnb_hbm,
            y_ref, k_ref, v_ref,
-           hid, normed, wkv, wq, wo, bq, seg, segcol, kv, q_s, o_all, part, m_s, l_s, acc_s,
+           hid, normed, wkv, wq, wo, bq_own, bq_pair, bkv_ref, bo_ref, gain_ref, lnb_ref, seg, segcol, kv, q_s, o_all, part, m_s, l_s, acc_s,
            load_sem, send_sem, o_send, bq_recv, seg_recv, kv_recv, wq_recv, wo_recv, o_recv):
     tok, d_model = hid.shape
     width = wq.shape[2]
@@ -67,9 +67,13 @@
     loads = [pltpu.make_async_copy(hid_hbm, hid, load_sem.at[0]),
              pltpu.make_async_copy(wkv_hbm, wkv, load_sem.at[1]),
              pltpu.make_async_copy(wq_hbm, wq.at[0], load_sem.at[2]),
-             pltpu.make_async_copy(bq_hbm, bq.at[0], load_sem.at[3]),
+             pltpu.make_async_copy(bq_hbm, bq_own, load_sem.at[3]),
              pltpu.make_async_copy(seg_hbm, seg.at[cp], load_sem.at[4]),
-             pltpu.make_async_copy(wo_hbm, wo.at[pl.ds(z * width, width), :], load_sem.at[5])]
+             pltpu.make_async_copy(wo_hbm, wo.at[pl.ds(z * width, width), :], load_sem.at[5]),
+             pltpu.make_async_copy(gain_hbm, gain_ref, load_sem.at[6]),
+             pltpu.make_async_copy(lnb_hbm, lnb_ref, load_sem.at[7]),
+             pltpu.make_async_copy(bkv_hbm, bkv_ref, load_sem.at[8]),
+             pltpu.make_async_copy(bo_hbm, bo_ref, load_sem.at[9])]
     for load in loads:
         load.start()
 
@@ -92,7 +96,7 @@
     wo_piece = lambda g, p: wo.at[pl.ds(g * width + p * o_rows, o_rows), :]
 
     own_q, own_o = lambda: wq_hbm.at[pl.ds(p_me * q_rows, q_rows), :], lambda: wo_hbm.at[pl.ds(p_me * o_rows, o_rows), :]
-    sends.go(lambda: bq_hbm, lambda: bq.at[1], lambda: bq_recv, {'tp': pair})
+    sends.go(lambda: bq_hbm, lambda: bq_pair, lambda: bq_recv, {'tp': pair})
     sends.go(own_q, lambda: wq_piece(p_me), lambda: wq_recv.at[p_me], {'tp': pair})
     sends.go(own_o, lambda: wo_piece(z, p_me), lambda: wo_recv.at[z, p_me], {'tp': z - 1}, lambda: z > 0)
     sends.go(own_o, lambda: wo_piece(z, p_me), lambda: wo_recv.at[z, p_me], {'tp': z + 1}, lambda: z < 3)
@@ -129,7 +133,8 @@
         for source in sources:
             pass_on(functools.partial(wo_piece, g), lambda p: wo_recv.at[g, p], source, g)
 
-    loads[0].wait()
+    for i in (0, 6, 7):
+        loads[i].wait()
     gain = gain_ref[...].astype(F32)
     lnb = lnb_ref[...].astype(F32)
     ln_rows = min(64, tok)
@@ -145,14 +150,15 @@
     lax.fori_loop(0, tok // ln_rows, ln_step, 0)
 
     loads[1].wait()
+    loads[8].wait()
     kv_new = (jnp.dot(normed[...], wkv[...], preferred_element_type=F32) + bkv_ref[...].astype(F32)).astype(BF16)
     kv[cp, 0] = kv_new[:, :HEAD_DIM]
     kv[cp, 1] = kv_new[:, HEAD_DIM:]
     k_ref[...] = kv_new[:, :HEAD_DIM]
     v_ref[...] = kv_new[:, HEAD_DIM:]
 
-    def project_q(which):
-        qf = jnp.dot(normed[...], wq[which], preferred_element_type=F32) + bq[which].astype(F32)
+    def project_q(which, bias):
+        qf = jnp.dot(normed[...], wq[which], preferred_element_type=F32) + bias[...].astype(F32)
         for r in range(4):
             for h in range(heads):
                 q_s[which * 4 + r, h * tile:(h + 1) * tile, :] = qf[r * tile:(r + 1) * tile, h * HEAD_DIM:(h + 1) * HEAD_DIM].astype(BF16)
@@ -161,7 +167,7 @@
     loads[3].wait()
     sends.go(lambda: kv.at[cp], lambda: kv.at[cp], lambda: kv_recv.at[cp], to_core, lambda: c == 0)
     sends.go(lambda: kv.at[cp], lambda: kv.at[cp], lambda: kv_recv.at[cp], to_y, lambda: y == 0)
-    project_q(0)
+    project_q(0, bq_own)
     loads[4].wait()
     for r in range(4):
         row = jnp.broadcast_to(seg[cp, :, r * tile:(r + 1) * tile], (tile, tile))
@@ -186,8 +192,8 @@
         @pl.when(t == 4)
         def _():
             from_core(wq_piece, lambda p: wq_recv.at[p])
-            arrived(bq.at[1], bq_recv)
-            project_q(1)
+            arrived(bq_pair, bq_recv)
+            project_q(1, bq_pair)
 
         q = q_s[t]
         seg_q = segcol[r][:, :1]
@@ -253,6 +259,7 @@
         lax.fori_loop(0, d_model // n_col, cols, 0)
 
     loads[5].wait()
+    loads[9].wait()
     every = pl.ds(0, tok)
     project_o(z, every, tok)
     from_core(functools.partial(wo_piece, g_a), lambda p: wo_recv.at[g_a, p])
@@ -321,15 +328,15 @@
         width = w_q.shape[1]
         heads = width // HEAD_DIM
         tile = tok // 4
-        hbm = pl.BlockSpec(memory_space=pl.ANY)
+        hbm = pl.BlockSpec(memory_space=pltpu.HBM)
         vmem = pl.BlockSpec(memory_space=pltpu.VMEM)
-        row = lambda a: a.reshape(1, -1)
         dma = pltpu.SemaphoreType.DMA
+        far = lambda a: pltpu.with_memory_space_constraint(a, pltpu.HBM)
         return pl.pallas_call(
             kernel,
             out_shape=(jax.ShapeDtypeStruct((tok, d_model), BF16), jax.ShapeDtypeStruct((tok, HEAD_DIM), BF16),
                        jax.ShapeDtypeStruct((tok, HEAD_DIM), BF16)),
-            in_specs=[hbm, hbm, hbm, hbm, hbm, vmem, hbm, vmem, vmem, vmem],
+            in_specs=[hbm] * 10,
             out_specs=(vmem, vmem, vmem),
             scratch_shapes=[
                 pltpu.VMEM((tok, d_model), BF16),
@@ -337,7 +344,12 @@
                 pltpu.VMEM((d_model, 2 * HEAD_DIM), BF16),
                 pltpu.VMEM((2, d_model, width), BF16),
                 pltpu.VMEM((4 * width, d_model), BF16),
-                pltpu.VMEM((2, 1, width), BF16),
+                pltpu.VMEM((width,), BF16),
+                pltpu.VMEM((width,), BF16),
+                pltpu.VMEM((2 * HEAD_DIM,), BF16),
+                pltpu.VMEM((d_model,), BF16),
+                pltpu.VMEM((d_model,), BF16),
+                pltpu.VMEM((d_model,), BF16),
                 pltpu.VMEM((4, 1, tok), jnp.int32),
                 pltpu.VMEM((4, tile, tile), jnp.int32),
                 pltpu.VMEM((4, 2, tok, HEAD_DIM), BF16),
@@ -347,11 +359,11 @@
                 pltpu.VMEM((heads * tile, HEAD_DIM), F32),
                 pltpu.VMEM((heads * tile, HEAD_DIM), F32),
                 pltpu.VMEM((heads * tile, HEAD_DIM), F32),
-                dma((6,)), dma((N_SENDS,)), dma((16,)), dma(()), dma((4,)), dma((4,)), dma((8,)), dma((4, 8)), dma((8,)),
+                dma((10,)), dma((N_SENDS,)), dma((16,)), dma(()), dma((4,)), dma((4,)), dma((8,)), dma((4, 8)), dma((8,)),
             ],
-            compiler_params=pltpu.CompilerParams(collective_id=0, has_side_effects=True, vmem_limit_bytes=60 * 2 ** 20),
+            compiler_params=pltpu.CompilerParams(collective_id=0, has_side_effects=True, vmem_limit_bytes=44 * 2 ** 20),
             name='block',
-        )(hidden, row(seg_ids), w_q, row(b_q), w_kv, row(b_kv), w_o, row(b_o), row(ln_gain), row(ln_bias))
+        )(far(hidden), far(seg_ids.reshape(1, -1)), far(w_q), far(b_q), far(w_kv), far(b_kv), far(w_o), far(b_o), far(ln_gain), far(ln_bias))
 
     row_spec = P(('dp', 'cp'), None)
     tok_spec = P(('dp', 'cp'))

time: 95.2 us -> 85.2 us (0.89)
  local copies, waits for them, and re-layouts: 10.9 us -> 2.63 us
  Pallas kernels: 83.3 us -> 81.8 us
    reshape x5 -> x0, local copies, waits for them, and re-layouts: 6.36 us -> none  [local_block(): row = lambda a: a.reshape(1, -1)]
    unnamed x7 -> x3, local copies, waits for them, and re-layouts: 4.52 us -> 2.63 us
    pallas_call x1, Pallas kernels: 83.3 us -> 81.8 us  [local_block(): pl.pallas_call(kernel, out_shape=(jax.ShapeDtypeStruct((tok, d_model), BF...]
where the time goes in v2:
time: 85.2 us; the launch traced here: 85.1 us
  Pallas kernels  81.8 us (96%)
  local copies, waits for them, and re-layouts  2.63 us (3%)
    pallas_call x1, Pallas kernels, local_block(): pl.pallas_call(kernel, out_shape=(jax.ShapeDtypeStruct((tok, d_model), BF...  81.8 us
    unnamed x3, local copies, waits for them, and re-layouts  2.63 us

profile of v2, /device:TPU:0, one launch (start us, length us, event | category | flops | bytes accessed | tf_op | source)
XLA Modules:
  0.0 85.1 jit_solution(3179318087150438256)
XLA Ops:
  0.6 81.8 %block.1 = (bf16[512,2048]{1,0:T(8,128)(2,1)S(1)}, bf16[512,128]{1,0:T(8,128)(2,1)S(1)}, bf16[512,128]{1,0:T(8,128)(2,1)S(1)}) custom-call(bf16[512,2048]{1,0:T(8,128)(2,1)} %hid_hbm.1, s32[1,512]{1,0:T(1,128)} %bitcast.1, bf16[2048,512]{1,0:T(8,128)(2,1)} %wq_hbm.1, bf16[512]{0:T(512)(128)(2,1)} %bq_hbm.1, bf16[2048,256]{1,0:T(8,128)(2,1)} %wkv_hbm.1, ...), custom_call_target="tpu_custom_call" | custom-call | tf_op jit(solution)/shard_map/block/pallas_call | solution.py:335
  82.4 1.3 %copy.16 = bf16[512,2048]{1,0:T(8,128)(2,1)} copy(bf16[512,2048]{1,0:T(8,128)(2,1)S(1)} %get-tuple-element.6) | data formatting | bytes 4194304
  83.7 0.7 copy.17
  84.4 0.7 copy.18
